TPU v7x, 32 devices: a whole 2x2x4 slice. The times are simulated.
32 devices in a mesh: unit: 4 (over y, core), ep: 4 (over z), fsdp: 2 (over x).
Axes of the slice: x: 2, y: 2, z: 4, core: 2. Of those that a mesh axis runs over, the one named last changes fastest.
Arguments:
- w_down: float32 [256, 1024, 2048], P(('unit', 'ep'), None, 'fsdp'), parts along dimension 0, may hold values from -0.25 to 0.25
- router_weight: float32 [8192, 64], P(('unit', 'fsdp'), 'ep'), parts along dimension 0, may hold values from -0.125 to 0.125
- router_gain: float32 [8192], P(('unit', 'fsdp')), parts along dimension 0, may hold values from 0.25 to 1.75
Outputs:
- serve_down: bfloat16 [256, 1024, 2048], P(('unit', 'ep'), 'fsdp'), parts along dimension 0
- scale_down: float32 [256, 1024], P(('unit', 'ep'), 'fsdp'), parts along dimension 0
- serve_router: bfloat16 [8192, 64], P('unit'), parts along dimension 0
There are 4 independent parts, one for each index of `unit`. A program takes and returns all parts, laid end to end along the dimension named above; each array names one. Nothing has to cross between parts.
All inputs are finite; a program needn't handle non-finite values. Where the computation divides by a largest or mean magnitude, that divisor is 1e-20 or more.
Results may differ from a plain program's by a relative error of at most 0.001.
Values may be sent and summed in bfloat16 or wider, within the bound.
A program may use at most 256 MiB of HBM per device.

v0:
```python
import jax
import jax.numpy as jnp
from jax import lax
from jax.sharding import PartitionSpec as P

D_MODEL = 2048


def on_device(w_down, router_weight, router_gain):
    total_down = lax.psum(jnp.sum(jnp.abs(w_down), axis=2), "fsdp")
    scale_down = total_down / D_MODEL
    narrow_down = (w_down / jnp.expand_dims(scale_down, 2)).astype(jnp.bfloat16)
    serve_down = lax.all_to_all(narrow_down, "fsdp", split_axis=1, concat_axis=2, tiled=True)
    scale_down = lax.dynamic_slice_in_dim(
        scale_down, lax.axis_index("fsdp") * serve_down.shape[1], serve_down.shape[1], axis=1
    )
    part_router = (router_weight * router_gain[:, None]).astype(jnp.bfloat16)
    row_router = lax.all_gather(part_router, "fsdp", axis=0, tiled=True)
    serve_router = lax.all_gather(row_router, "ep", axis=1, tiled=True)
    return (serve_down, scale_down, serve_router)


def solution(mesh):
    return jax.shard_map(
        on_device,
        mesh=mesh,
        in_specs=(P(("unit", "ep"), None, "fsdp"), P(("unit", "fsdp"), "ep"), P(("unit", "fsdp"))),
        out_specs=(P(("unit", "ep"), "fsdp", None), P(("unit", "ep"), "fsdp"), P("unit", None)),
        check_vma=False,
    )
```

profile of v0, /device:TPU:0, one launch (start us, length us, event | category | flops | bytes accessed | tf_op | source)
XLA Modules:
  0.0 625.7 jit_solution(12388147618959563152)
XLA Ops:
  7.2 0.0 all-reduce.2.cloned.1.call-start
  7.2 21.4 %abs_reduce_fusion = f32[16,1024]{1,0:T(8,128)} fusion(f32[16,1024,1024]{2,1,0:T(8,128)} %param.3), kind=kLoop, calls=%fused_computation.2 | loop fusion | flops 33538048 | bytes 67174400 | tf_op jit(solution)/shard_map/reduce_sum | solution.py:10
  28.6 0.0 all-reduce.2.cloned.1.call-update
  28.7 23.8 %all-reduce.2.cloned.1.call-done = f32[16,1024]{1,0:T(8,128)} async-done(((f32[16,1024]{1,0:T(8,128)}), f32[16,1024]{1,0:T(8,128)}) %all-reduce.2.cloned.1.call-update) | async-done | bytes 65552 | tf_op jit(solution)/shard_map/psum | solution.py:10
  52.5 0.8 broadcast_multiply_fusion
  53.3 0.2 copy.7
  53.5 0.0 copy-start
  53.5 0.0 copy-start.1
  53.6 60.1 %fusion = bf16[16,1024,1024]{2,0,1:T(8,128)(2,1)} fusion(f32[16,1024,1024]{2,1,0:T(8,128)} %param.3, f32[16,1024]{0,1:T(8,128)S(1)} %copy.7), kind=kLoop, calls=%fused_computation.1 | loop fusion | flops 33554432 | bytes 100728832 | tf_op jit(solution)/shard_map/convert_element_type | solution.py:12
  113.7 13.0 %all-to-all-start = ((bf16[16,1024,1024]{2,0,1:T(8,128)(2,1)}), bf16[16,1024,1024]{2,0,1:T(8,128)(2,1)}, u32[]{:S(2)}, u32[]{:S(2)}) async-start(bf16[16,1024,1024]{2,0,1:T(8,128)(2,1)} %fusion), calls=%async_computation | async-start | bytes 67108864 | tf_op jit(solution)/shard_map/all_to_all | solution.py:13
  126.6 0.0 copy-done
  126.6 0.0 copy-done.1
  126.7 362.4 %all_gather.6 = bf16[2048,16]{0,1:T(8,128)(2,1)S(1)} all-gather(bf16[1024,16]{0,1:T(8,128)(2,1)S(1)} %multiply_convert_fusion), channel_id=1, replica_groups=mesh['unit'=4,'ep'=4,'fsdp'=2] {'fsdp'}, dimensions={0}, use_global_device_ids=true | all-gather | bytes 98304 | tf_op jit(solution)/shard_map/all_gather | solution.py:18
  489.0 13.8 %all_gather.7 = bf16[2048,64]{0,1:T(8,128)(2,1)S(1)} all-gather(bf16[2048,16]{0,1:T(8,128)(2,1)S(1)} %all_gather.6), channel_id=1, replica_groups=mesh['unit'=4,'ep'=4,'fsdp'=2] {'ep'}, dimensions={1}, use_global_device_ids=true | all-gather | bytes 327680 | tf_op jit(solution)/shard_map/all_gather | solution.py:19
  502.9 0.6 constant_dynamic-slice_fusion
  503.5 0.0 all-to-all-done
  503.5 60.5 %copy.9 = bf16[16,512,2,1024]{3,2,1,0:T(2,128)(2,1)} copy(bf16[16,512,2,1024]{3,0,1,2:T(8,128)(2,1)} %bitcast.1) | data formatting | bytes 67108864 | tf_op jit(solution)/shard_map/all_to_all | solution.py:13
  564.0 54.2 %all_to_all.16 = bf16[16,512,2048]{2,1,0:T(8,128)(2,1)} reshape(bf16[16,512,2,1024]{3,2,1,0:T(2,128)(2,1)} %copy.9) | data formatting | bytes 67108864 | tf_op jit(solution)/shard_map/all_to_all | solution.py:13
  618.2 0.7 copy.15
  (1 shorter events, 0.0 us)
Async XLA Ops:
  7.2 45.3 %all-reduce.2.cloned.1.call-start = ((), (), s32[]{:S(2)}) async-start(), calls=%async_computation.1 | async-start | bytes 131072 | tf_op jit(solution)/shard_map/psum | solution.py:10
  53.5 73.1 %copy-start = (f32[1024,16]{0,1:T(8,128)S(1)}, f32[1024,16]{0,1:T(8,128)}, u32[]{:S(2)}) copy-start(f32[1024,16]{0,1:T(8,128)} %param.4) | copy-start | bytes 196612
  53.5 73.1 %copy-start.1 = (f32[1024]{0:T(1024)S(1)}, f32[1024]{0:T(1024)}, u32[]{:S(2)}) copy-start(f32[1024]{0:T(1024)} %param.5) | copy-start | bytes 12292
  113.7 389.8 %all-to-all-start = ((bf16[16,1024,1024]{2,0,1:T(8,128)(2,1)}), bf16[16,1024,1024]{2,0,1:T(8,128)(2,1)}, u32[]{:S(2)}, u32[]{:S(2)}) async-start(bf16[16,1024,1024]{2,0,1:T(8,128)(2,1)} %fusion), calls=%async_computation | async-start | bytes 67108864 | tf_op jit(solution)/shard_map/all_to_all | solution.py:13
Sparse Core Ops, SparseCore 0:
  28.8 23.6 all-reduce.1
where the time goes:
time: 627 us; the launch traced here: 626 us
  blocking collectives  376 us (60%)
  local copies, waits for them, and re-layouts  116 us (19%)
  other arithmetic  82.4 us (13%)
  waiting for transfers between devices  23.9 us (4%)
  between operations  14.1 us (2%)
  starting transfers between devices  13 us (2%)
    all_gather x1, blocking collectives, on_device(): row_router = lax.all_gather(part_router, 'fsdp', axis=0, tiled=True)  362 us
    all_to_all x2, local copies, waits for them, and re-layouts, on_device(): lax.all_to_all(narrow_down, 'fsdp', split_axis=1, concat_axis=2, tiled=True)  115 us
    convert_element_type x1, other arithmetic, on_device(): narrow_down = (w_down / jnp.expand_dims(scale_down, 2)).astype(jnp.bfloat16)  60.1 us
    psum x1, waiting for transfers between devices, on_device(): total_down = lax.psum(jnp.sum(jnp.abs(w_down), axis=2), 'fsdp')  23.8 us
    reduce_sum x1, other arithmetic, on_device(): total_down = lax.psum(jnp.sum(jnp.abs(w_down), axis=2), 'fsdp')  21.4 us
    all_gather x1, blocking collectives, on_device(): serve_router = lax.all_gather(row_router, 'ep', axis=1, tiled=True)  13.8 us
    all_to_all x1, starting transfers between devices, on_device(): lax.all_to_all(narrow_down, 'fsdp', split_axis=1, concat_axis=2, tiled=True)  13 us
  transfers between devices with their start and end apart: 2, of which 1 were waited for; matrix products, arithmetic and copies ran while one was open for 0% of the time, Pallas kernels for 0%

commit v1 on v0

--- a/solution.py
+++ b/solution.py
@@ -10,7 +10,9 @@
     total_down = lax.psum(jnp.sum(jnp.abs(w_down), axis=2), "fsdp")
     scale_down = total_down / D_MODEL
     narrow_down = (w_down / jnp.expand_dims(scale_down, 2)).astype(jnp.bfloat16)
-    serve_down = lax.all_to_all(narrow_down, "fsdp", split_axis=1, concat_axis=2, tiled=True)
+    pieces = jnp.split(narrow_down, lax.axis_size("fsdp"), axis=1)
+    incoming = lax.all_to_all(jnp.stack(pieces), "fsdp", 0, 0)
+    serve_down = jnp.concatenate(incoming, axis=2)
     scale_down = lax.dynamic_slice_in_dim(
         scale_down, lax.axis_index("fsdp") * serve_down.shape[1], serve_down.shape[1], axis=1
     )

time: 627 us -> 553 us (0.88)
  local copies, waits for them, and re-layouts: 116 us -> 47.7 us
    all_to_all x2 -> x0, local copies, waits for them, and re-layouts: 115 us -> none  [on_device(): lax.all_to_all(narrow_down, 'fsdp', split_axis=1, concat_axis=2, tiled=True)]
    convert_element_type x1, other arithmetic: 60.1 us -> 32.9 us  [on_device(): narrow_down = (w_down / jnp.expand_dims(scale_down, 2)).astype(jnp.bfloat16)]
    reshape x0 -> x1, local copies, waits for them, and re-layouts: none -> 23.3 us  [on_device(): serve_down = jnp.concatenate(incoming, axis=2)]
    another operation x0 -> x1, local copies, waits for them, and re-layouts: none -> 23.1 us  [on_device(): incoming = lax.all_to_all(jnp.stack(pieces), 'fsdp', 0, 0)]
    another operation x0 -> x1, other arithmetic: none -> 23 us  [on_device(): incoming = lax.all_to_all(jnp.stack(pieces), 'fsdp', 0, 0)]
where the time goes in v1:
time: 553 us
  blocking collectives  376 us (68%)
  other arithmetic  78.1 us (14%)
  local copies, waits for them, and re-layouts  47.7 us (9%)
  waiting for transfers between devices  23.9 us (4%)
  between operations  14.1 us (3%)
  starting transfers between devices  13.1 us (2%)
    all_gather x1, blocking collectives, on_device(): row_router = lax.all_gather(part_router, 'fsdp', axis=0, tiled=True)  362 us
    convert_element_type x1, other arithmetic, on_device(): narrow_down = (w_down / jnp.expand_dims(scale_down, 2)).astype(jnp.bfloat16)  32.9 us
    psum x1, waiting for transfers between devices, on_device(): total_down = lax.psum(jnp.sum(jnp.abs(w_down), axis=2), 'fsdp')  23.8 us
    reshape x1, local copies, waits for them, and re-layouts, on_device(): serve_down = jnp.concatenate(incoming, axis=2)  23.3 us
    another operation x1, local copies, waits for them, and re-layouts, on_device(): incoming = lax.all_to_all(jnp.stack(pieces), 'fsdp', 0, 0)  23.1 us
    another operation x1, other arithmetic, on_device(): incoming = lax.all_to_all(jnp.stack(pieces), 'fsdp', 0, 0)  23 us
    reduce_sum x1, other arithmetic, on_device(): total_down = lax.psum(jnp.sum(jnp.abs(w_down), axis=2), 'fsdp')  21.4 us
    all_gather x1, blocking collectives, on_device(): serve_router = lax.all_gather(row_router, 'ep', axis=1, tiled=True)  13.8 us
  transfers between devices with their start and end apart: 2, of which 1 were waited for; matrix products, arithmetic and copies ran while one was open for 0% of the time, Pallas kernels for 0%

profile of v1, /device:TPU:0, one launch (start us, length us, event | category | flops | bytes accessed | tf_op | source)
XLA Modules:
  0.0 553.1 jit_solution(2984466817001409051)
XLA Ops:
  7.2 0.0 all-reduce.2.cloned.1.call-start
  7.2 21.4 %abs_reduce_fusion = f32[16,1024]{1,0:T(8,128)} fusion(f32[16,1024,1024]{2,1,0:T(8,128)} %param.3), kind=kLoop, calls=%fused_computation.1 | loop fusion | flops 33538048 | bytes 67174400 | tf_op jit(solution)/shard_map/reduce_sum | solution.py:10
  28.6 0.0 all-reduce.2.cloned.1.call-update
  28.7 23.8 %all-reduce.2.cloned.1.call-done = f32[16,1024]{1,0:T(8,128)} async-done(((f32[16,1024]{1,0:T(8,128)}), f32[16,1024]{1,0:T(8,128)}) %all-reduce.2.cloned.1.call-update) | async-done | bytes 65552 | tf_op jit(solution)/shard_map/psum | solution.py:10
  52.5 0.8 broadcast_multiply_fusion
  53.3 32.9 %divide_convert_fusion = bf16[16,1024,1024]{2,1,0:T(8,128)(2,1)} fusion(f32[16,1024,1024]{2,1,0:T(8,128)} %param.3, f32[16,1024]{1,0:T(8,128)S(1)} %broadcast_multiply_fusion), kind=kLoop, calls=%fused_computation | loop fusion | flops 33554432 | bytes 100728832 | tf_op jit(solution)/shard_map/convert_element_type | solution.py:12
  86.2 23.1 %slice_bitcast_fusion.1 = (bf16[1,16,512,1024]{3,2,1,0:T(8,128)(2,1)}, bf16[1,16,512,1024]{3,2,1,0:T(8,128)(2,1)}) fusion(bf16[16,1024,1024]{2,1,0:T(8,128)(2,1)} %divide_convert_fusion), kind=kLoop, calls=%fused_computation.4 | loop fusion | bytes 67108864 | tf_op jit(solution)/shard_map/stack | solution.py:14
  109.3 23.0 %pad_maximum_fusion = bf16[2,16,512,1024]{3,2,1,0:T(8,128)(2,1)} fusion(bf16[1,16,512,1024]{3,2,1,0:T(8,128)(2,1)} %get-tuple-element.4, bf16[1,16,512,1024]{3,2,1,0:T(8,128)(2,1)} %get-tuple-element.3), kind=kLoop, calls=%fused_computation.2 | loop fusion | flops 16777216 | bytes 67108864 | tf_op jit(solution)/shard_map/stack | solution.py:14
  132.3 0.0 copy-start
  132.3 0.0 copy-start.1
  132.3 13.1 %all-to-all-start = ((bf16[2,16,512,1024]{3,2,1,0:T(8,128)(2,1)}), bf16[2,16,512,1024]{3,2,1,0:T(8,128)(2,1)}, u32[]{:S(2)}, u32[]{:S(2)}) async-start(bf16[2,16,512,1024]{3,2,1,0:T(8,128)(2,1)} %pad_maximum_fusion), calls=%async_computation | async-start | bytes 67108864 | tf_op jit(solution)/shard_map/all_to_all | solution.py:14
  145.4 0.0 copy-done
  145.4 0.0 copy-done.1
  145.5 362.4 %all_gather.6 = bf16[2048,16]{0,1:T(8,128)(2,1)S(1)} all-gather(bf16[1024,16]{0,1:T(8,128)(2,1)S(1)} %multiply_convert_fusion), channel_id=1, replica_groups=mesh['unit'=4,'ep'=4,'fsdp'=2] {'fsdp'}, dimensions={0}, use_global_device_ids=true | all-gather | bytes 98304 | tf_op jit(solution)/shard_map/all_gather | solution.py:20
  507.8 13.8 %all_gather.7 = bf16[2048,64]{0,1:T(8,128)(2,1)S(1)} all-gather(bf16[2048,16]{0,1:T(8,128)(2,1)S(1)} %all_gather.6), channel_id=1, replica_groups=mesh['unit'=4,'ep'=4,'fsdp'=2] {'ep'}, dimensions={1}, use_global_device_ids=true | all-gather | bytes 327680 | tf_op jit(solution)/shard_map/all_gather | solution.py:21
  521.7 0.6 constant_dynamic-slice_fusion
  522.3 0.0 all-to-all-done
  522.3 23.3 %copy.7 = bf16[2,16,64,8,1024]{4,3,0,2,1:T(8,128)(2,1)} copy(bf16[2,16,64,8,1024]{4,3,2,1,0:T(8,128)(2,1)} %bitcast.3) | data formatting | bytes 67108864 | tf_op jit(solution)/shard_map/reshape | solution.py:15
  545.6 0.7 copy.10
  (1 shorter events, 0.0 us)
Async XLA Ops:
  7.2 45.3 %all-reduce.2.cloned.1.call-start = ((), (), s32[]{:S(2)}) async-start(), calls=%async_computation.1 | async-start | bytes 131072 | tf_op jit(solution)/shard_map/psum | solution.py:10
  132.3 13.1 %copy-start = (f32[1024,16]{0,1:T(8,128)S(1)}, f32[1024,16]{0,1:T(8,128)}, u32[]{:S(2)}) copy-start(f32[1024,16]{0,1:T(8,128)} %param.4) | copy-start | bytes 196612
  132.3 13.1 %copy-start.1 = (f32[1024]{0:T(1024)S(1)}, f32[1024]{0:T(1024)}, u32[]{:S(2)}) copy-start(f32[1024]{0:T(1024)} %param.5) | copy-start | bytes 12292
  132.3 390.0 %all-to-all-start = ((bf16[2,16,512,1024]{3,2,1,0:T(8,128)(2,1)}), bf16[2,16,512,1024]{3,2,1,0:T(8,128)(2,1)}, u32[]{:S(2)}, u32[]{:S(2)}) async-start(bf16[2,16,512,1024]{3,2,1,0:T(8,128)(2,1)} %pad_maximum_fusion), calls=%async_computation | async-start | bytes 67108864 | tf_op jit(solution)/shard_map/all_to_all | solution.py:14
Sparse Core Ops, SparseCore 0:
  28.8 23.6 all-reduce.1
